TPU v7x, 128 devices: a whole 4x4x4 slice. The times are simulated.
128 devices in a mesh: head: 8 (over y, z_lo), ctx: 16 (over z_hi, x, core).
Axes of the slice: x: 4, y: 4, z: 4 (z_hi: 2, z_lo: 2; z = z_hi * 2 + z_lo), core: 2. Of those that a mesh axis runs over, the one named last changes fastest.
Arguments:
- query: bfloat16 [12288, 4096], P(('ctx', 'head')), may hold values from -8 to 8
- key: bfloat16 [12288, 2048], P(('ctx', 'head')), may hold values from -8 to 8
- value: bfloat16 [12288, 2048], P(('ctx', 'head')), may hold values from -8 to 8
- block_order: int32 [32], replicated, may hold values from 0 to 31, each once
Outputs:
- attended: bfloat16 [12288, 4096], P('ctx', 'head')
Inputs may be any that keep to these rules, and one draw needn't show every extreme that they name: `block_order`: each storage block index 0 to 31 appears exactly once.
All inputs are finite; a program needn't handle non-finite values.
Results may differ from a plain program's by a relative error of at most 0.0049.
Values may be sent and summed in bfloat16 or wider, within the bound.
No kernel may reach another device: no remote copies, remote signals or barrier semaphores. Data moves between devices by JAX's collectives and lax.ppermute only.
A program may use at most 128 MiB of HBM per device.

v0:
```python
import functools

import jax
import jax.numpy as jnp
from jax import lax
from jax.experimental import pallas as pl
from jax.experimental.pallas import tpu as pltpu
from jax.sharding import Mesh
from jax.sharding import PartitionSpec as P

HEAD = 128
BLK = 384
PIECE = 96
TILE = 256
UNROLL = 4
SCORE_SCALE = 1.0 / (12.0 * 50.0)
CAP_LOG2E = 50.0 * 1.4426950408889634

AXES = ("y", "zlo", "zhi", "x", "core")
REMOTE, LOCAL, BOTH = 0, 1, 2
SLOTS = tuple((half, yhi, flip) for half in (REMOTE, LOCAL) for yhi in range(2) for flip in range(2))


def slots_of(half):
    return tuple(slot for slot in SLOTS if half in (slot[0], BOTH))


def attend_kernel(*refs, offsets, half, first, last, split):
    slots = slots_of(half)
    blocks = len(slots)
    tiles = blocks * BLK // TILE
    refs = list(refs)
    order = refs.pop(0)
    kv = [refs.pop(0) for _ in offsets]
    if first:
        q_refs = [refs.pop(0) for _ in range(2)]
    else:
        state_in = [refs.pop(0) for _ in range(3)]
    if last and half == REMOTE:
        both = refs.pop(0)
        outs = [both.at[0], both.at[1]]
    elif last:
        outs = [refs.pop(0) for _ in range(2)]
    else:
        states_out = [[refs.pop(0) for _ in range(3)] for _ in range(2 if split else 1)]
    qt, num, den, qpos, kbuf, vt = refs[:6]
    s_bufs = refs[6 : 6 + UNROLL]
    p_bufs = refs[6 + UNROLL : 6 + 2 * UNROLL]
    rows, q_seq, q_rank, kb_list, kb_start, kb_seq = refs[6 + 2 * UNROLL :]

    x = lax.axis_index("x")
    core = lax.axis_index("core")
    zhi = lax.axis_index("zhi")

    seqs = []
    for side, yhi, flip in slots:
        zz = 1 - zhi if side == REMOTE else zhi
        cc = 1 - core if flip else core
        seqs.append(order[2 * (zz * 8 + x * 2 + cc) + yhi])

    def rank_among(slot, others):
        rank = jnp.int32(0)
        for other in others:
            if other != slot:
                rank = rank + (seqs[other] < seqs[slot]).astype(jnp.int32)
        return rank

    for slot in range(blocks):
        rank = rank_among(slot, range(blocks))
        q_seq[rank] = seqs[slot]
        q_rank[slot] = rank
    lane = lax.broadcasted_iota(jnp.int32, (8, 128), 1)
    for g in range(2 * tiles):
        base = q_seq[g // 3] * BLK + (g % 3) * 128
        qpos[g // 2, :, (g % 2) * 128 : (g % 2) * 128 + 128] = lane + base
    qpos[tiles] = jnp.zeros((8, TILE), jnp.int32)

    if first:
        for slot, (side, yhi, flip) in enumerate(slots):
            zz = 1 - zhi if side == REMOTE else zhi
            top = pl.multiple_of(q_rank[slot] * BLK, BLK)
            for sub in range(4):
                piece = q_refs[flip][yhi * 8 + sub * 2 + zz]
                rows[pl.ds(top + sub * PIECE, PIECE), :] = piece
        for t in range(tiles):
            qt[t] = rows[t * TILE : (t + 1) * TILE, :].T
            num[t] = jnp.zeros((HEAD, TILE), jnp.float32)
            den[t] = jnp.zeros((8, TILE), jnp.float32)
    else:
        for t in range(tiles):
            qt[t] = state_in[0][t]
            num[t] = state_in[1][t]
            den[t] = state_in[2][t]
    qt[tiles] = jnp.zeros((HEAD, TILE), jnp.bfloat16)
    num[tiles] = jnp.zeros((HEAD, TILE), jnp.float32)
    den[tiles] = jnp.zeros((8, TILE), jnp.float32)

    count = jnp.int32(0)
    total = jnp.int32(0)
    for n, (dx, flip, yhi) in enumerate(offsets):
        xs = (x + (4 - dx)) % 4
        cs = 1 - core if flip else core
        for zz in range(2):
            kb = 2 * n + zz
            vals = []
            for sub in range(4):
                piece = kv[n][sub * 2 + zz]
                kbuf[kb, sub * PIECE : (sub + 1) * PIECE, :] = piece[:, :HEAD]
                vals.append(piece[:, HEAD:])
            vt[kb] = jnp.concatenate(vals, axis=0).T
            seq = order[2 * (zz * 8 + xs * 2 + cs) + yhi]
            below = jnp.int32(0)
            for slot in range(blocks):
                below = below + (seqs[slot] < seq).astype(jnp.int32)
            start = (3 * below) // 2
            kb_list[count] = jnp.int32(kb)
            kb_start[count] = start
            kb_seq[count] = seq
            count = count + (start < tiles).astype(jnp.int32)
            total = total + (tiles - start)
    for extra in range(2 * UNROLL + 2):
        kb_list[count + extra] = jnp.int32(0)
        kb_start[count + extra] = jnp.int32(tiles)
        kb_seq[count + extra] = jnp.int32(0)

    def after(item):
        j, t = item
        wrap = t + 1 >= tiles
        j = jnp.where(wrap, j + 1, j)
        return j, jnp.where(wrap, kb_start[j], t + 1)

    def score(item, s):
        j, t = item
        s[...] = jnp.dot(kbuf[kb_list[j]], qt[t], preferred_element_type=jnp.float32)

    row = lax.broadcasted_iota(jnp.int32, (8, TILE), 0)

    def weigh(item, s, p):
        j, t = item
        rel = qpos[t] - (kb_seq[j] * BLK + row)
        acc = None
        for r in range(0, BLK, 16):
            both = []
            for h in range(2):
                z = s[r + 8 * h : r + 8 * h + 8, :]
                w = jnp.exp2(CAP_LOG2E * jnp.tanh(z * SCORE_SCALE))
                w = jnp.where(rel >= r + 8 * h, w, 0.0)
                acc = w if acc is None else acc + w
                both.append(w)
            p[r : r + 16, :] = jnp.concatenate(both, axis=0).astype(jnp.bfloat16)
        den[t] = den[t] + acc

    def gather(item, p):
        j, t = item
        num[t] = num[t] + jnp.dot(vt[kb_list[j]], p[...], preferred_element_type=jnp.float32)

    items = [(jnp.int32(0), kb_start[0])]
    for _ in range(UNROLL - 1):
        items.append(after(items[-1]))
    for k in range(UNROLL):
        score(items[k], s_bufs[k])
    p_bufs[UNROLL - 1][...] = jnp.zeros((BLK, TILE), jnp.bfloat16)

    def body(_, state):
        cur, prev = state
        nxt = []
        item = cur[-1]
        for _ in range(UNROLL):
            item = after(item)
            nxt.append(item)
        weigh(cur[0], s_bufs[0], p_bufs[0])
        weigh(cur[1], s_bufs[1], p_bufs[1])
        gather(prev, p_bufs[3])
        score(nxt[0], s_bufs[0])
        score(nxt[1], s_bufs[1])
        gather(cur[0], p_bufs[0])
        weigh(cur[2], s_bufs[2], p_bufs[2])
        score(nxt[2], s_bufs[2])
        weigh(cur[3], s_bufs[3], p_bufs[3])
        gather(cur[1], p_bufs[1])
        gather(cur[2], p_bufs[2])
        score(nxt[3], s_bufs[3])
        return tuple(nxt), cur[-1]

    idle = (count, jnp.int32(tiles))
    _, tail = lax.fori_loop(0, (total + UNROLL - 1) // UNROLL, body, (tuple(items), idle))
    gather(tail, p_bufs[UNROLL - 1])

    if last:
        for t in range(tiles):
            inv = 1.0 / jnp.sum(den[t], axis=0, keepdims=True)
            rows[t * TILE : (t + 1) * TILE, :] = (num[t] * inv).T.astype(jnp.bfloat16)
        for slot, (_, yhi, flip) in enumerate(slots):
            top = pl.multiple_of(q_rank[slot] * BLK, BLK)
            outs[flip][yhi * BLK : (yhi + 1) * BLK, :] = rows[pl.ds(top, BLK), :]
    elif split:
        for slot in range(blocks):
            mates = range(0, 4) if slot < 4 else range(4, 8)
            to = rank_among(slot, mates) * 3
            at = q_rank[slot] * 3
            for j in range(3):
                source = pl.ds(pl.multiple_of(((at + j) % 2) * 128, 128), 128)
                target = pl.ds(pl.multiple_of(((to + j) % 2) * 128, 128), 128)
                for out, held in zip(states_out[slot // 4], (qt, num, den)):
                    out[(to + j) // 2, :, target] = held[(at + j) // 2, :, source]
    else:
        for t in range(tiles):
            for out, held in zip(states_out[0], (qt, num, den)):
                out[t] = held[t]


def attend(order, given, half, carry, first, last, split):
    kvs = [piece for piece, _, _, _ in given]
    offsets = tuple(at for _, *at in given)
    vmem = pl.BlockSpec(memory_space=pltpu.VMEM)
    smem = pl.BlockSpec(memory_space=pltpu.SMEM)
    nb = 2 * len(given)
    blocks = len(slots_of(half))
    tiles = blocks * BLK // TILE
    runs = nb + 2 * UNROLL + 4
    if last and half == REMOTE:
        out = (jax.ShapeDtypeStruct((2, 2 * BLK, HEAD), jnp.bfloat16),)
    elif last:
        out = (jax.ShapeDtypeStruct((2 * BLK, HEAD), jnp.bfloat16),) * 2
    else:
        kept = tiles // 2 if split else tiles
        out = (
            jax.ShapeDtypeStruct((kept, HEAD, TILE), jnp.bfloat16),
            jax.ShapeDtypeStruct((kept, HEAD, TILE), jnp.float32),
            jax.ShapeDtypeStruct((kept, 8, TILE), jnp.float32),
        ) * (2 if split else 1)
    inputs = [order, *kvs, *carry]
    return pl.pallas_call(
        functools.partial(
            attend_kernel, offsets=offsets, half=half, first=first, last=last, split=split
        ),
        out_shape=out,
        in_specs=[smem] + [vmem] * (len(inputs) - 1),
        out_specs=(vmem,) * len(out),
        scratch_shapes=[
            pltpu.VMEM((tiles + 1, HEAD, TILE), jnp.bfloat16),
            pltpu.VMEM((tiles + 1, HEAD, TILE), jnp.float32),
            pltpu.VMEM((tiles + 1, 8, TILE), jnp.float32),
            pltpu.VMEM((tiles + 1, 8, TILE), jnp.int32),
            pltpu.VMEM((nb, BLK, HEAD), jnp.bfloat16),
            pltpu.VMEM((nb, HEAD, BLK), jnp.bfloat16),
            *[pltpu.VMEM((BLK, TILE), jnp.float32) for _ in range(UNROLL)],
            *[pltpu.VMEM((BLK, TILE), jnp.bfloat16) for _ in range(UNROLL)],
            pltpu.VMEM((tiles * TILE, HEAD), jnp.bfloat16),
            pltpu.SMEM((blocks,), jnp.int32),
            pltpu.SMEM((blocks,), jnp.int32),
            pltpu.SMEM((runs,), jnp.int32),
            pltpu.SMEM((runs,), jnp.int32),
            pltpu.SMEM((runs,), jnp.int32),
        ],
        compiler_params=pltpu.CompilerParams(vmem_limit_bytes=28 * 1024 * 1024),
        cost_estimate=pl.CostEstimate(
            flops=len(given) * blocks * 150_000_000,
            transcendentals=0,
            bytes_accessed=4_000_000,
        ),
    )(*inputs)


def local_call(body, outs, inputs):
    vmem = pl.BlockSpec(memory_space=pltpu.VMEM)
    return pl.pallas_call(
        body,
        out_shape=tuple(jax.ShapeDtypeStruct(shape, jnp.bfloat16) for shape in outs),
        in_specs=[vmem] * len(inputs),
        out_specs=(vmem,) * len(outs),
        compiler_params=pltpu.CompilerParams(vmem_limit_bytes=8 * 1024 * 1024),
    )(*inputs)


def sort_kernel(query, key, value, out, q_rows, k_rows, v_rows, packed, sems):
    copies = [
        pltpu.make_async_copy(source, rows, sems.at[n])
        for n, (source, rows) in enumerate(((query, q_rows), (key, k_rows), (value, v_rows)))
    ]
    for copy in copies:
        copy.start()
    for copy in copies:
        copy.wait()
    for head in range(16):
        packed[head, :, : 2 * HEAD] = q_rows[:, 2 * head * HEAD : 2 * (head + 1) * HEAD]
        packed[head, :, 2 * HEAD : 3 * HEAD] = k_rows[:, head * HEAD : (head + 1) * HEAD]
        packed[head, :, 3 * HEAD :] = v_rows[:, head * HEAD : (head + 1) * HEAD]
    done = pltpu.make_async_copy(packed, out, sems.at[3])
    done.start()
    done.wait()


def split_kernel(got, low, high, keep, send):
    core = lax.axis_index("core")
    mine = pl.multiple_of(core * HEAD, HEAD)
    other = pl.multiple_of((1 - core) * HEAD, HEAD)
    for n in range(16):
        (low, high)[n // 8][n % 8] = got[n, :, 2 * HEAD :]
        keep[n] = got[n, :, pl.ds(mine, HEAD)]
        send[n] = got[n, :, pl.ds(other, HEAD)]


def assemble_kernel(own, swapped, across, across_o, out):
    zhi = lax.axis_index("zhi")
    core = lax.axis_index("core")
    for piece, zz, cc in (
        (across.at[0], 1 - zhi, core),
        (across_o.at[1], 1 - zhi, 1 - core),
        (own, zhi, core),
        (swapped, zhi, 1 - core),
    ):
        left = pl.multiple_of((zz * 2 + cc) * HEAD, HEAD)
        out[:, pl.ds(left, HEAD)] = piece[...]


def along(value, axis, by):
    return lax.ppermute(value, axis, [(i, (i + by) % 4) for i in range(4)])


def mirror(value, axes):
    size = 2 if isinstance(axes, str) else 4
    return lax.ppermute(value, axes, [(i, size - 1 - i) for i in range(size)])


def layer(query, key, value, block_order):
    rows = query.shape[0]
    packed = pl.pallas_call(
        sort_kernel,
        out_shape=jax.ShapeDtypeStruct((16, rows, 4 * HEAD), jnp.bfloat16),
        in_specs=[pl.BlockSpec(memory_space=pltpu.HBM)] * 3,
        out_specs=pl.BlockSpec(memory_space=pltpu.HBM),
        scratch_shapes=[
            pltpu.VMEM(query.shape, jnp.bfloat16),
            pltpu.VMEM(key.shape, jnp.bfloat16),
            pltpu.VMEM(value.shape, jnp.bfloat16),
            pltpu.VMEM((16, rows, 4 * HEAD), jnp.bfloat16),
            pltpu.SemaphoreType.DMA((4,)),
        ],
        compiler_params=pltpu.CompilerParams(vmem_limit_bytes=62 * 1024 * 1024),
        name="k_sort",
    )(query, key, value)
    packed = lax.all_to_all(packed, ("y", "zlo", "zhi"), 0, 0)
    low, high, keep, send = local_call(
        split_kernel, [(8, rows, 2 * HEAD)] * 2 + [(16, rows, HEAD)] * 2, (packed,)
    )
    got = mirror(send, "core")
    up_low = along(low, "x", 1)
    down_high = along(high, "x", -1)
    up_high = along(high, "x", 1)
    down_low = along(low, "x", -1)
    far_low = along(up_low, "x", 1)
    far_high = along(down_high, "x", -1)

    def swap(half):
        return mirror(half, "core")

    own = [(low, 0, 0, 0), (high, 0, 0, 1)]
    own += [(swap(low), 0, 1, 0), (swap(high), 0, 1, 1)]
    near = [(up_low, 1, 0, 0), (down_high, 3, 0, 1)]
    near += [(swap(up_low), 1, 1, 0), (swap(down_high), 3, 1, 1)]
    rest = [(up_high, 1, 0, 1), (down_low, 3, 0, 0), (far_low, 2, 0, 0), (far_high, 2, 0, 1)]
    rest_o = [(swap(up_high), 1, 1, 1), (swap(down_low), 3, 1, 0)]
    rest_o += [(swap(far_low), 2, 1, 0), (swap(far_high), 2, 1, 1)]

    def step(given, half, carry, first=False, last=False, split=False):
        return attend(block_order, given, half, carry, first, last, split)

    state = step(own, BOTH, (keep, got), first=True)
    state = step(near, BOTH, state, split=True)
    remote, local = state[:3], state[3:]
    remote = step(rest, REMOTE, remote)
    (sent,) = step(rest_o, REMOTE, remote, last=True)
    across = mirror(sent, "zhi")
    mine, cross = step(rest + rest_o, LOCAL, local, last=True)
    swapped = mirror(cross, "core")
    across_o = mirror(across, "core")
    (out,) = local_call(assemble_kernel, [(2 * BLK, 4 * HEAD)], (mine, swapped, across, across_o))
    return out


def solution(mesh):
    fine = Mesh(mesh.devices.reshape(4, 2, 2, 4, 2), AXES)
    placed = P(("zhi", "x", "core", "y", "zlo"), None)
    return jax.shard_map(
        layer,
        mesh=fine,
        in_specs=(placed, placed, placed, P()),
        out_specs=P(("zhi", "x", "core"), ("y", "zlo")),
        check_vma=False,
    )
```

profile of v0, /device:TPU:5, one launch (start us, length us, event | category | flops | bytes accessed | tf_op | source)
XLA Modules:
  0.0 119.0 jit_solution(7810164096131107822)
XLA Ops:
  0.0 2.7 %k_sort.1 = bf16[16,96,512]{2,1,0:T(8,128)(2,1)} custom-call(bf16[96,4096]{1,0:T(8,128)(2,1)} %query.1, bf16[96,2048]{1,0:T(8,128)(2,1)} %key.1, bf16[96,2048]{1,0:T(8,128)(2,1)} %value.1), custom_call_target="tpu_custom_call" | custom-call | tf_op jit(solution)/shard_map/k_sort/pallas_call | solution.py:328
  2.7 29.6 %all_to_all.5.got = bf16[16,96,512]{2,1,0:T(8,128)(2,1)S(1)} all-to-all(bf16[16,96,512]{2,1,0:T(8,128)(2,1)} %k_sort.1), channel_id=1, replica_groups=mesh['y'=4,'zlo'=2,'zhi'=2,'x'=4,'core'=2] {'y','zlo','zhi'}, dimensions={0} | all-to-all | bytes 3145728 | tf_op jit(solution)/shard_map/all_to_all | solution.py:343
  32.4 0.0 copy-start
  32.4 0.2 shard_map.46
  32.5 2.1 %collective-permute-start.12 = (bf16[8,96,256]{2,1,0:T(8,128)(2,1)S(1)}, bf16[8,96,256]{2,1,0:T(8,128)(2,1)S(1)}, u32[]{:S(2)}, u32[]{:S(2)}) collective-permute-start(bf16[8,96,256]{2,1,0:T(8,128)(2,1)S(1)} %get-tuple-element.24.refs_1_), channel_id=1, source_target_pairs={{0,1},{1,0},{2,3},{3,2},{4,5},{5,4},{6,7},{7,6},{8,9},{9,8},{10,11... | collective-permute-start | bytes 1179656 | tf_op jit(solution)/shard_map/ppermute | solution.py:323
  34.6 0.1 collective-permute-start.13
  34.7 0.9 collective-permute-start.2
  35.6 0.7 collective-permute-start.14
  36.3 0.5 collective-permute-start.4
  36.9 0.0 collective-permute-done.12.refs_3_
  36.9 0.9 collective-permute-start
  37.8 0.0 collective-permute-done.13.refs_4_
  37.8 0.5 collective-permute-start.1
  38.4 6.6 %collective-permute-done.2.refs_1_ = bf16[8,96,256]{2,1,0:T(8,128)(2,1)S(1)} collective-permute-done((bf16[8,96,256]{2,1,0:T(8,128)(2,1)S(1)}, bf16[8,96,256]{2,1,0:T(8,128)(2,1)S(1)}, u32[]{:S(2)}, u32[]{:S(2)}) %collective-permute-start.2) | collective-permute-done | bytes 393248 | tf_op jit(solution)/shard_map/ppermute | solution.py:318
  45.0 2.1 %collective-permute-start.10 = (bf16[8,96,256]{2,1,0:T(8,128)(2,1)S(1)}, bf16[8,96,256]{2,1,0:T(8,128)(2,1)S(1)}, u32[]{:S(2)}, u32[]{:S(2)}) collective-permute-start(bf16[8,96,256]{2,1,0:T(8,128)(2,1)S(1)} %collective-permute-done.2.refs_1_), channel_id=1, source_target_pairs={{0,1},{1,0},{2,3},{3,2},{4,5},{5,4},{6,7},{7,6},{8,9},{9,8},{10,11... | collective-permute-start | bytes 1179656 | tf_op jit(solution)/shard_map/ppermute | solution.py:323
  47.1 0.0 collective-permute-done.14.refs_6_
  47.1 0.9 collective-permute-start.3
  48.0 0.0 collective-permute-done.4.refs_2_
  48.0 0.3 collective-permute-start.11
  48.3 5.1 %collective-permute-done.refs_1_ = bf16[8,96,256]{2,1,0:T(8,128)(2,1)S(1)} collective-permute-done((bf16[8,96,256]{2,1,0:T(8,128)(2,1)S(1)}, bf16[8,96,256]{2,1,0:T(8,128)(2,1)S(1)}, u32[]{:S(2)}, u32[]{:S(2)}) %collective-permute-start) | collective-permute-done | bytes 393248 | tf_op jit(solution)/shard_map/ppermute | solution.py:318
  53.4 0.3 collective-permute-start.5
  53.7 0.0 copy-done
  53.7 9.7 %shard_map.47 = (bf16[12,128,256]{2,1,0:T(8,128)(2,1)S(1)}, f32[12,128,256]{2,1,0:T(8,128)S(1)}, f32[12,8,256]{2,1,0:T(8,128)S(1)}) custom-call(s32[32]{0:T(128)S(1)} %copy-done, bf16[8,96,256]{2,1,0:T(8,128)(2,1)S(1)} %get-tuple-element.24.refs_1_, bf16[8,96,256]{2,1,0:T(8,128)(2,1)S(1)} %get-tuple-element.23.refs_2_, ...), custom_call_target="tpu_custom_call" | custom-call | flops 4800000000 | bytes 4000000 | tf_op jit(solution)/shard_map/pallas_call | solution.py:233
  63.3 0.0 collective-permute-done.1.refs_2_
  63.3 2.5 %collective-permute-start.6 = (bf16[8,96,256]{2,1,0:T(8,128)(2,1)S(1)}, bf16[8,96,256]{2,1,0:T(8,128)(2,1)S(1)}, u32[]{:S(2)}, u32[]{:S(2)}) collective-permute-start(bf16[8,96,256]{2,1,0:T(8,128)(2,1)S(1)} %collective-permute-done.refs_1_), channel_id=1, source_target_pairs={{0,1},{1,0},{2,3},{3,2},{4,5},{5,4},{6,7},{7,6},{8,9},{9,8},{10,11... | collective-permute-start | bytes 1179656 | tf_op jit(solution)/shard_map/ppermute | solution.py:323
  65.8 0.0 collective-permute-done.10.refs_3_
  65.8 0.1 collective-permute-start.7
  65.9 0.0 collective-permute-done.3.refs_3_
  65.9 0.4 collective-permute-start.8
  66.4 0.0 collective-permute-done.5.refs_4_
  66.4 0.1 collective-permute-start.9
  66.5 0.0 collective-permute-done.11.refs_4_
  66.5 11.1 %shard_map.48 = (bf16[6,128,256]{2,1,0:T(8,128)(2,1)S(1)}, f32[6,128,256]{2,1,0:T(8,128)S(1)}, f32[6,8,256]{2,1,0:T(8,128)S(1)}, bf16[6,128,256]{2,1,0:T(8,128)(...) custom-call(s32[32]{0:T(128)S(1)} %copy-done, bf16[8,96,256]{2,1,0:T(8,128)(2,1)S(1)} %collective-permute-done.2.refs_1_, ...), custom_call_target="tpu_custom_call" | custom-call | flops 4800000000 | bytes 4000000 | tf_op jit(solution)/shard_map/pallas_call | solution.py:233
  77.6 5.8 %shard_map.50 = (bf16[6,128,256]{2,1,0:T(8,128)(2,1)S(1)}, f32[6,128,256]{2,1,0:T(8,128)S(1)}, f32[6,8,256]{2,1,0:T(8,128)S(1)}) custom-call(s32[32]{0:T(128)S(1)} %copy-done, bf16[8,96,256]{2,1,0:T(8,128)(2,1)S(1)} %collective-permute-done.refs_1_, bf16[8,96,256]{2,1,0:T(8,128)(2,1)S(1)} %collective-permute-done.1.refs_2_, ...), custom_call_target="tpu_custom_call" | custom-call | flops 2400000000 | bytes 4000000 | tf_op jit(solution)/shard_map/pallas_call | solution.py:233
  83.4 0.0 collective-permute-done.6.refs_5_.refs_1_
  83.4 0.0 collective-permute-done.7.refs_6_.refs_2_
  83.4 0.0 collective-permute-done.8.refs_7_.refs_3_
  83.4 0.0 collective-permute-done.9.refs_8_.refs_4_
  83.4 7.2 %shard_map.51 = bf16[2,768,128]{2,1,0:T(8,128)(2,1)S(1)} custom-call(s32[32]{0:T(128)S(1)} %copy-done, bf16[8,96,256]{2,1,0:T(8,128)(2,1)S(1)} %collective-permute-done.6.refs_5_.refs_1_, bf16[8,96,256]{2,1,0:T(8,128)(2,1)S(1)} %collective-permute-done.7.refs_6_.refs_2_, bf16[8,96,256]{2,1,0:T(8,128)(2,1)S(1)} %collective-permute-done.8.refs_7_.refs_3_, ...), custom_call_target="tpu_custom_call" | custom-call | flops 2400000000 | bytes 4000000 | tf_op jit(solution)/shard_map/pallas_call | solution.py:233
  90.6 1.6 %collective-permute-start.16 = (bf16[2,768,128]{2,1,0:T(8,128)(2,1)S(1)}, bf16[2,768,128]{2,1,0:T(8,128)(2,1)S(1)}, u32[]{:S(2)}, u32[]{:S(2)}) collective-permute-start(bf16[2,768,128]{2,1,0:T(8,128)(2,1)S(1)} %shard_map.51), channel_id=1, source_target_pairs={{0,8},{8,0},{1,9},{9,1},{2,10},{10,2},{3,11},{11,3},{4,12},{12,4},... | collective-permute-start | bytes 1179656 | tf_op jit(solution)/shard_map/ppermute | solution.py:323
  92.2 10.3 %collective-permute-done.16.across = bf16[2,768,128]{2,1,0:T(8,128)(2,1)S(1)} collective-permute-done((bf16[2,768,128]{2,1,0:T(8,128)(2,1)S(1)}, bf16[2,768,128]{2,1,0:T(8,128)(2,1)S(1)}, u32[]{:S(2)}, u32[]{:S(2)}) %collective-permute-start.16) | collective-permute-done | bytes 393248 | tf_op jit(solution)/shard_map/ppermute | solution.py:323
  102.4 1.3 %collective-permute-start.17 = (bf16[2,768,128]{2,1,0:T(8,128)(2,1)S(1)}, bf16[2,768,128]{2,1,0:T(8,128)(2,1)S(1)}, u32[]{:S(2)}, u32[]{:S(2)}) collective-permute-start(bf16[2,768,128]{2,1,0:T(8,128)(2,1)S(1)} %collective-permute-done.16.across), channel_id=1, source_target_pairs={{0,1},{1,0},{2,3},{3,2},{4,5},{5,4},{6,7},{7,6},{8,9},{9,8},{10,11... | collective-permute-start | bytes 1179656 | tf_op jit(solution)/shard_map/ppermute | solution.py:323
  103.7 12.7 %shard_map.49 = (bf16[768,128]{1,0:T(8,128)(2,1)S(1)}, bf16[768,128]{1,0:T(8,128)(2,1)S(1)}) custom-call(s32[32]{0:T(128)S(1)} %copy-done, bf16[8,96,256]{2,1,0:T(8,128)(2,1)S(1)} %collective-permute-done.refs_1_, bf16[8,96,256]{2,1,0:T(8,128)(2,1)S(1)} %collective-permute-done.1.refs_2_, bf16[8,96,256]{2,1,0:T(8,128)(2,1)S(1)} %collective-permute-done.3.refs_3_, ...), custom_call_target="tpu_custom_call" | custom-call | flops 4800000000 | bytes 4000000 | tf_op jit(solution)/shard_map/pallas_call | solution.py:233
  116.4 0.1 collective-permute-start.15
  116.5 1.4 %collective-permute-done.15.swapped = bf16[768,128]{1,0:T(8,128)(2,1)S(1)} collective-permute-done((bf16[768,128]{1,0:T(8,128)(2,1)S(1)}, bf16[768,128]{1,0:T(8,128)(2,1)S(1)}, u32[]{:S(2)}, u32[]{:S(2)}) %collective-permute-start.15) | collective-permute-done | bytes 196640 | tf_op jit(solution)/shard_map/ppermute | solution.py:323
  117.9 0.0 collective-permute-done.17.across_o
  117.9 1.1 shard_map.52
Async XLA Ops:
  32.4 21.3 %copy-start = (s32[32]{0:T(128)S(1)}, s32[32]{0:T(128)}, u32[]{:S(2)}) copy-start(s32[32]{0:T(128)} %refs_0_.9) | copy-start | bytes 388
  32.5 4.3 %collective-permute-start.12 = (bf16[8,96,256]{2,1,0:T(8,128)(2,1)S(1)}, bf16[8,96,256]{2,1,0:T(8,128)(2,1)S(1)}, u32[]{:S(2)}, u32[]{:S(2)}) collective-permute-start(bf16[8,96,256]{2,1,0:T(8,128)(2,1)S(1)} %get-tuple-element.24.refs_1_), channel_id=1, source_target_pairs={{0,1},{1,0},{2,3},{3,2},{4,5},{5,4},{6,7},{7,6},{8,9},{9,8},{10,11... | collective-permute-start | bytes 1179656 | tf_op jit(solution)/shard_map/ppermute | solution.py:323
  34.6 3.2 %collective-permute-start.13 = (bf16[8,96,256]{2,1,0:T(8,128)(2,1)S(1)}, bf16[8,96,256]{2,1,0:T(8,128)(2,1)S(1)}, u32[]{:S(2)}, u32[]{:S(2)}) collective-permute-start(bf16[8,96,256]{2,1,0:T(8,128)(2,1)S(1)} %get-tuple-element.23.refs_2_), channel_id=1, source_target_pairs={{0,1},{1,0},{2,3},{3,2},{4,5},{5,4},{6,7},{7,6},{8,9},{9,8},{10,11... | collective-permute-start | bytes 1179656 | tf_op jit(solution)/shard_map/ppermute | solution.py:323
  34.7 10.3 %collective-permute-start.2 = (bf16[8,96,256]{2,1,0:T(8,128)(2,1)S(1)}, bf16[8,96,256]{2,1,0:T(8,128)(2,1)S(1)}, u32[]{:S(2)}, u32[]{:S(2)}) collective-permute-start(bf16[8,96,256]{2,1,0:T(8,128)(2,1)S(1)} %get-tuple-element.24.refs_1_), channel_id=1, source_target_pairs={{0,2},{2,4},{4,6},{6,0},{1,3},{3,5},{5,7},{7,1},{8,10},{10,12},{12... | collective-permute-start | bytes 1179656 | tf_op jit(solution)/shard_map/ppermute | solution.py:318
  35.6 11.5 %collective-permute-start.14 = (bf16[16,96,128]{2,1,0:T(8,128)(2,1)S(1)}, bf16[16,96,128]{2,1,0:T(8,128)(2,1)S(1)}, u32[]{:S(2)}, u32[]{:S(2)}) collective-permute-start(bf16[16,96,128]{2,1,0:T(8,128)(2,1)S(1)} %get-tuple-element.26), channel_id=1, source_target_pairs={{0,1},{1,0},{2,3},{3,2},{4,5},{5,4},{6,7},{7,6},{8,9},{9,8},{10,11... | collective-permute-start | bytes 1179656 | tf_op jit(solution)/shard_map/ppermute | solution.py:323
  36.3 11.7 %collective-permute-start.4 = (bf16[8,96,256]{2,1,0:T(8,128)(2,1)S(1)}, bf16[8,96,256]{2,1,0:T(8,128)(2,1)S(1)}, u32[]{:S(2)}, u32[]{:S(2)}) collective-permute-start(bf16[8,96,256]{2,1,0:T(8,128)(2,1)S(1)} %get-tuple-element.23.refs_2_), channel_id=1, source_target_pairs={{0,6},{2,0},{4,2},{6,4},{1,7},{3,1},{5,3},{7,5},{8,14},{10,8},{12,... | collective-permute-start | bytes 1179656 | tf_op jit(solution)/shard_map/ppermute | solution.py:318
  36.9 16.5 %collective-permute-start = (bf16[8,96,256]{2,1,0:T(8,128)(2,1)S(1)}, bf16[8,96,256]{2,1,0:T(8,128)(2,1)S(1)}, u32[]{:S(2)}, u32[]{:S(2)}) collective-permute-start(bf16[8,96,256]{2,1,0:T(8,128)(2,1)S(1)} %get-tuple-element.23.refs_2_), channel_id=1, source_target_pairs={{0,2},{2,4},{4,6},{6,0},{1,3},{3,5},{5,7},{7,1},{8,10},{10,12},{12... | collective-permute-start | bytes 1179656 | tf_op jit(solution)/shard_map/ppermute | solution.py:318
  37.8 25.5 %collective-permute-start.1 = (bf16[8,96,256]{2,1,0:T(8,128)(2,1)S(1)}, bf16[8,96,256]{2,1,0:T(8,128)(2,1)S(1)}, u32[]{:S(2)}, u32[]{:S(2)}) collective-permute-start(bf16[8,96,256]{2,1,0:T(8,128)(2,1)S(1)} %get-tuple-element.24.refs_1_), channel_id=1, source_target_pairs={{0,6},{2,0},{4,2},{6,4},{1,7},{3,1},{5,3},{7,5},{8,14},{10,8},{12,... | collective-permute-start | bytes 1179656 | tf_op jit(solution)/shard_map/ppermute | solution.py:318
  45.0 20.9 %collective-permute-start.10 = (bf16[8,96,256]{2,1,0:T(8,128)(2,1)S(1)}, bf16[8,96,256]{2,1,0:T(8,128)(2,1)S(1)}, u32[]{:S(2)}, u32[]{:S(2)}) collective-permute-start(bf16[8,96,256]{2,1,0:T(8,128)(2,1)S(1)} %collective-permute-done.2.refs_1_), channel_id=1, source_target_pairs={{0,1},{1,0},{2,3},{3,2},{4,5},{5,4},{6,7},{7,6},{8,9},{9,8},{10,11... | collective-permute-start | bytes 1179656 | tf_op jit(solution)/shard_map/ppermute | solution.py:323
  47.1 18.8 %collective-permute-start.3 = (bf16[8,96,256]{2,1,0:T(8,128)(2,1)S(1)}, bf16[8,96,256]{2,1,0:T(8,128)(2,1)S(1)}, u32[]{:S(2)}, u32[]{:S(2)}) collective-permute-start(bf16[8,96,256]{2,1,0:T(8,128)(2,1)S(1)} %collective-permute-done.2.refs_1_), channel_id=1, source_target_pairs={{0,2},{2,4},{4,6},{6,0},{1,3},{3,5},{5,7},{7,1},{8,10},{10,12},{12... | collective-permute-start | bytes 1179656 | tf_op jit(solution)/shard_map/ppermute | solution.py:318
  48.0 18.4 %collective-permute-start.11 = (bf16[8,96,256]{2,1,0:T(8,128)(2,1)S(1)}, bf16[8,96,256]{2,1,0:T(8,128)(2,1)S(1)}, u32[]{:S(2)}, u32[]{:S(2)}) collective-permute-start(bf16[8,96,256]{2,1,0:T(8,128)(2,1)S(1)} %collective-permute-done.4.refs_2_), channel_id=1, source_target_pairs={{0,1},{1,0},{2,3},{3,2},{4,5},{5,4},{6,7},{7,6},{8,9},{9,8},{10,11... | collective-permute-start | bytes 1179656 | tf_op jit(solution)/shard_map/ppermute | solution.py:323
  53.4 13.0 %collective-permute-start.5 = (bf16[8,96,256]{2,1,0:T(8,128)(2,1)S(1)}, bf16[8,96,256]{2,1,0:T(8,128)(2,1)S(1)}, u32[]{:S(2)}, u32[]{:S(2)}) collective-permute-start(bf16[8,96,256]{2,1,0:T(8,128)(2,1)S(1)} %collective-permute-done.4.refs_2_), channel_id=1, source_target_pairs={{0,6},{2,0},{4,2},{6,4},{1,7},{3,1},{5,3},{7,5},{8,14},{10,8},{12,... | collective-permute-start | bytes 1179656 | tf_op jit(solution)/shard_map/ppermute | solution.py:318
  63.3 20.0 %collective-permute-start.6 = (bf16[8,96,256]{2,1,0:T(8,128)(2,1)S(1)}, bf16[8,96,256]{2,1,0:T(8,128)(2,1)S(1)}, u32[]{:S(2)}, u32[]{:S(2)}) collective-permute-start(bf16[8,96,256]{2,1,0:T(8,128)(2,1)S(1)} %collective-permute-done.refs_1_), channel_id=1, source_target_pairs={{0,1},{1,0},{2,3},{3,2},{4,5},{5,4},{6,7},{7,6},{8,9},{9,8},{10,11... | collective-permute-start | bytes 1179656 | tf_op jit(solution)/shard_map/ppermute | solution.py:323
  65.8 17.6 %collective-permute-start.7 = (bf16[8,96,256]{2,1,0:T(8,128)(2,1)S(1)}, bf16[8,96,256]{2,1,0:T(8,128)(2,1)S(1)}, u32[]{:S(2)}, u32[]{:S(2)}) collective-permute-start(bf16[8,96,256]{2,1,0:T(8,128)(2,1)S(1)} %collective-permute-done.1.refs_2_), channel_id=1, source_target_pairs={{0,1},{1,0},{2,3},{3,2},{4,5},{5,4},{6,7},{7,6},{8,9},{9,8},{10,11... | collective-permute-start | bytes 1179656 | tf_op jit(solution)/shard_map/ppermute | solution.py:323
  65.9 17.5 %collective-permute-start.8 = (bf16[8,96,256]{2,1,0:T(8,128)(2,1)S(1)}, bf16[8,96,256]{2,1,0:T(8,128)(2,1)S(1)}, u32[]{:S(2)}, u32[]{:S(2)}) collective-permute-start(bf16[8,96,256]{2,1,0:T(8,128)(2,1)S(1)} %collective-permute-done.3.refs_3_), channel_id=1, source_target_pairs={{0,1},{1,0},{2,3},{3,2},{4,5},{5,4},{6,7},{7,6},{8,9},{9,8},{10,11... | collective-permute-start | bytes 1179656 | tf_op jit(solution)/shard_map/ppermute | solution.py:323
  66.4 17.1 %collective-permute-start.9 = (bf16[8,96,256]{2,1,0:T(8,128)(2,1)S(1)}, bf16[8,96,256]{2,1,0:T(8,128)(2,1)S(1)}, u32[]{:S(2)}, u32[]{:S(2)}) collective-permute-start(bf16[8,96,256]{2,1,0:T(8,128)(2,1)S(1)} %collective-permute-done.5.refs_4_), channel_id=1, source_target_pairs={{0,1},{1,0},{2,3},{3,2},{4,5},{5,4},{6,7},{7,6},{8,9},{9,8},{10,11... | collective-permute-start | bytes 1179656 | tf_op jit(solution)/shard_map/ppermute | solution.py:323
  90.6 11.8 %collective-permute-start.16 = (bf16[2,768,128]{2,1,0:T(8,128)(2,1)S(1)}, bf16[2,768,128]{2,1,0:T(8,128)(2,1)S(1)}, u32[]{:S(2)}, u32[]{:S(2)}) collective-permute-start(bf16[2,768,128]{2,1,0:T(8,128)(2,1)S(1)} %shard_map.51), channel_id=1, source_target_pairs={{0,8},{8,0},{1,9},{9,1},{2,10},{10,2},{3,11},{11,3},{4,12},{12,4},... | collective-permute-start | bytes 1179656 | tf_op jit(solution)/shard_map/ppermute | solution.py:323
  102.4 15.5 %collective-permute-start.17 = (bf16[2,768,128]{2,1,0:T(8,128)(2,1)S(1)}, bf16[2,768,128]{2,1,0:T(8,128)(2,1)S(1)}, u32[]{:S(2)}, u32[]{:S(2)}) collective-permute-start(bf16[2,768,128]{2,1,0:T(8,128)(2,1)S(1)} %collective-permute-done.16.across), channel_id=1, source_target_pairs={{0,1},{1,0},{2,3},{3,2},{4,5},{5,4},{6,7},{7,6},{8,9},{9,8},{10,11... | collective-permute-start | bytes 1179656 | tf_op jit(solution)/shard_map/ppermute | solution.py:323
  116.4 1.5 %collective-permute-start.15 = (bf16[768,128]{1,0:T(8,128)(2,1)S(1)}, bf16[768,128]{1,0:T(8,128)(2,1)S(1)}, u32[]{:S(2)}, u32[]{:S(2)}) collective-permute-start(bf16[768,128]{1,0:T(8,128)(2,1)S(1)} %get-tuple-element.34), channel_id=1, source_target_pairs={{0,1},{1,0},{2,3},{3,2},{4,5},{5,4},{6,7},{7,6},{8,9},{9,8},{10,11... | collective-permute-start | bytes 589832 | tf_op jit(solution)/shard_map/ppermute | solution.py:323
where the time goes:
time: 119 us
  Pallas kernels  50.4 us (42%)
  blocking collectives  29.6 us (25%)
  waiting for transfers between devices  23.4 us (20%)
  starting transfers between devices  15.5 us (13%)
    pallas_call x5, Pallas kernels, attend(): pl.pallas_call(functools.partial(attend_kernel, offsets=offsets, half=hal...  46.4 us
    all_to_all x1, blocking collectives, layer(): packed = lax.all_to_all(packed, ('y', 'zlo', 'zhi'), 0, 0)  29.6 us
    ppermute x12, waiting for transfers between devices, mirror(): return lax.ppermute(value, axes, [(i, size - 1 - i) for i in range(size)])  11.7 us
    ppermute x6, waiting for transfers between devices, along(): return lax.ppermute(value, axis, [(i, (i + by) % 4) for i in range(4)])  11.7 us
    ppermute x12, starting transfers between devices, mirror(): return lax.ppermute(value, axes, [(i, size - 1 - i) for i in range(size)])  11.4 us
    ppermute x6, starting transfers between devices, along(): return lax.ppermute(value, axis, [(i, (i + by) % 4) for i in range(4)])  4.11 us
    pallas_call x1, Pallas kernels, layer(): pl.pallas_call(sort_kernel, out_shape=jax.ShapeDtypeStruct((16, rows, 4 *...  2.72 us
  transfers between devices with their start and end apart: 18, of which 4 were waited for; matrix products, arithmetic and copies ran while one was open for 0% of the time, Pallas kernels for 33%

commit v1 on v0

--- a/solution.py
+++ b/solution.py
@@ -36,10 +36,7 @@
         q_refs = [refs.pop(0) for _ in range(2)]
     else:
         state_in = [refs.pop(0) for _ in range(3)]
-    if last and half == REMOTE:
-        both = refs.pop(0)
-        outs = [both.at[0], both.at[1]]
-    elif last:
+    if last:
         outs = [refs.pop(0) for _ in range(2)]
     else:
         states_out = [[refs.pop(0) for _ in range(3)] for _ in range(2 if split else 1)]
@@ -218,9 +215,7 @@
     blocks = len(slots_of(half))
     tiles = blocks * BLK // TILE
     runs = nb + 2 * UNROLL + 4
-    if last and half == REMOTE:
-        out = (jax.ShapeDtypeStruct((2, 2 * BLK, HEAD), jnp.bfloat16),)
-    elif last:
+    if last:
         out = (jax.ShapeDtypeStruct((2 * BLK, HEAD), jnp.bfloat16),) * 2
     else:
         kept = tiles // 2 if split else tiles
@@ -301,12 +296,12 @@
         send[n] = got[n, :, pl.ds(other, HEAD)]
 
 
-def assemble_kernel(own, swapped, across, across_o, out):
+def assemble_kernel(own, swapped, z_same, z_cross, out):
     zhi = lax.axis_index("zhi")
     core = lax.axis_index("core")
     for piece, zz, cc in (
-        (across.at[0], 1 - zhi, core),
-        (across_o.at[1], 1 - zhi, 1 - core),
+        (z_same, 1 - zhi, core),
+        (z_cross, 1 - zhi, 1 - core),
         (own, zhi, core),
         (swapped, zhi, 1 - core),
     ):
@@ -370,12 +365,12 @@
     state = step(near, BOTH, state, split=True)
     remote, local = state[:3], state[3:]
     remote = step(rest, REMOTE, remote)
-    (sent,) = step(rest_o, REMOTE, remote, last=True)
-    across = mirror(sent, "zhi")
+    same, cross = step(rest_o, REMOTE, remote, last=True)
+    z_same = mirror(same, "zhi")
+    z_cross = mirror(cross, ("zhi", "core"))
     mine, cross = step(rest + rest_o, LOCAL, local, last=True)
     swapped = mirror(cross, "core")
-    across_o = mirror(across, "core")
-    (out,) = local_call(assemble_kernel, [(2 * BLK, 4 * HEAD)], (mine, swapped, across, across_o))
+    (out,) = local_call(assemble_kernel, [(2 * BLK, 4 * HEAD)], (mine, swapped, z_same, z_cross))
     return out
 
 

time: 119 us -> 110 us (0.924)
  waiting for transfers between devices: 23.4 us -> 13.1 us
    ppermute x12, waiting for transfers between devices: 11.7 us -> 1.44 us  [mirror(): return lax.ppermute(value, axes, [(i, size - 1 - i) for i in range(size)])]
  transfers between devices with their start and end apart: 18 -> 18, of which waited for: 4 -> 3; matrix products, arithmetic and copies ran while one was open for 0% -> 0% of each run, Pallas kernels for 33% -> 36%
where the time goes in v1:
time: 110 us
  Pallas kernels  50.4 us (46%)
  blocking collectives  29.6 us (27%)
  starting transfers between devices  16.3 us (15%)
  waiting for transfers between devices  13.1 us (12%)
    pallas_call x5, Pallas kernels, attend(): pl.pallas_call(functools.partial(attend_kernel, offsets=offsets, half=hal...  46.4 us
    all_to_all x1, blocking collectives, layer(): packed = lax.all_to_all(packed, ('y', 'zlo', 'zhi'), 0, 0)  29.6 us
    ppermute x12, starting transfers between devices, mirror(): return lax.ppermute(value, axes, [(i, size - 1 - i) for i in range(size)])  12.2 us
    ppermute x6, waiting for transfers between devices, along(): return lax.ppermute(value, axis, [(i, (i + by) % 4) for i in range(4)])  11.7 us
    ppermute x6, starting transfers between devices, along(): return lax.ppermute(value, axis, [(i, (i + by) % 4) for i in range(4)])  4.11 us
    pallas_call x1, Pallas kernels, layer(): pl.pallas_call(sort_kernel, out_shape=jax.ShapeDtypeStruct((16, rows, 4 *...  2.72 us
  transfers between devices with their start and end apart: 18, of which 3 were waited for; matrix products, arithmetic and copies ran while one was open for 0% of the time, Pallas kernels for 36%

profile of v1, /device:TPU:5, one launch (start us, length us, event | category | flops | bytes accessed | tf_op | source)
XLA Modules:
  0.0 109.6 jit_solution(4980171965925903486)
XLA Ops:
  0.0 2.7 %k_sort.1 = bf16[16,96,512]{2,1,0:T(8,128)(2,1)} custom-call(bf16[96,4096]{1,0:T(8,128)(2,1)} %query.1, bf16[96,2048]{1,0:T(8,128)(2,1)} %key.1, bf16[96,2048]{1,0:T(8,128)(2,1)} %value.1), custom_call_target="tpu_custom_call" | custom-call | tf_op jit(solution)/shard_map/k_sort/pallas_call | solution.py:323
  2.7 29.6 %all_to_all.5.got = bf16[16,96,512]{2,1,0:T(8,128)(2,1)S(1)} all-to-all(bf16[16,96,512]{2,1,0:T(8,128)(2,1)} %k_sort.1), channel_id=1, replica_groups=mesh['y'=4,'zlo'=2,'zhi'=2,'x'=4,'core'=2] {'y','zlo','zhi'}, dimensions={0} | all-to-all | bytes 3145728 | tf_op jit(solution)/shard_map/all_to_all | solution.py:338
  32.3 0.0 copy-start
  32.3 0.2 shard_map.46
  32.5 2.1 %collective-permute-start.12 = (bf16[8,96,256]{2,1,0:T(8,128)(2,1)S(1)}, bf16[8,96,256]{2,1,0:T(8,128)(2,1)S(1)}, u32[]{:S(2)}, u32[]{:S(2)}) collective-permute-start(bf16[8,96,256]{2,1,0:T(8,128)(2,1)S(1)} %get-tuple-element.26.refs_1_), channel_id=1, source_target_pairs={{0,1},{1,0},{2,3},{3,2},{4,5},{5,4},{6,7},{7,6},{8,9},{9,8},{10,11... | collective-permute-start | bytes 1179656 | tf_op jit(solution)/shard_map/ppermute | solution.py:318
  34.6 0.1 collective-permute-start.13
  34.7 0.9 collective-permute-start.2
  35.6 0.7 collective-permute-start.14
  36.3 0.5 collective-permute-start.4
  36.9 0.0 collective-permute-done.12.refs_3_
  36.9 0.9 collective-permute-start
  37.8 0.0 collective-permute-done.13.refs_4_
  37.8 0.5 collective-permute-start.1
  38.4 6.6 %collective-permute-done.2.refs_1_ = bf16[8,96,256]{2,1,0:T(8,128)(2,1)S(1)} collective-permute-done((bf16[8,96,256]{2,1,0:T(8,128)(2,1)S(1)}, bf16[8,96,256]{2,1,0:T(8,128)(2,1)S(1)}, u32[]{:S(2)}, u32[]{:S(2)}) %collective-permute-start.2) | collective-permute-done | bytes 393248 | tf_op jit(solution)/shard_map/ppermute | solution.py:313
  45.0 2.1 %collective-permute-start.10 = (bf16[8,96,256]{2,1,0:T(8,128)(2,1)S(1)}, bf16[8,96,256]{2,1,0:T(8,128)(2,1)S(1)}, u32[]{:S(2)}, u32[]{:S(2)}) collective-permute-start(bf16[8,96,256]{2,1,0:T(8,128)(2,1)S(1)} %collective-permute-done.2.refs_1_), channel_id=1, source_target_pairs={{0,1},{1,0},{2,3},{3,2},{4,5},{5,4},{6,7},{7,6},{8,9},{9,8},{10,11... | collective-permute-start | bytes 1179656 | tf_op jit(solution)/shard_map/ppermute | solution.py:318
  47.1 0.0 collective-permute-done.14.refs_6_
  47.1 0.9 collective-permute-start.3
  48.0 0.0 collective-permute-done.4.refs_2_
  48.0 0.3 collective-permute-start.11
  48.3 5.1 %collective-permute-done.refs_1_ = bf16[8,96,256]{2,1,0:T(8,128)(2,1)S(1)} collective-permute-done((bf16[8,96,256]{2,1,0:T(8,128)(2,1)S(1)}, bf16[8,96,256]{2,1,0:T(8,128)(2,1)S(1)}, u32[]{:S(2)}, u32[]{:S(2)}) %collective-permute-start) | collective-permute-done | bytes 393248 | tf_op jit(solution)/shard_map/ppermute | solution.py:313
  53.4 0.3 collective-permute-start.5
  53.7 0.0 copy-done
  53.7 9.7 %shard_map.47 = (bf16[12,128,256]{2,1,0:T(8,128)(2,1)S(1)}, f32[12,128,256]{2,1,0:T(8,128)S(1)}, f32[12,8,256]{2,1,0:T(8,128)S(1)}) custom-call(s32[32]{0:T(128)S(1)} %copy-done, bf16[8,96,256]{2,1,0:T(8,128)(2,1)S(1)} %get-tuple-element.26.refs_1_, bf16[8,96,256]{2,1,0:T(8,128)(2,1)S(1)} %get-tuple-element.25.refs_2_, ...), custom_call_target="tpu_custom_call" | custom-call | flops 4800000000 | bytes 4000000 | tf_op jit(solution)/shard_map/pallas_call | solution.py:228
  63.3 0.0 collective-permute-done.1.refs_2_
  63.3 2.5 %collective-permute-start.6 = (bf16[8,96,256]{2,1,0:T(8,128)(2,1)S(1)}, bf16[8,96,256]{2,1,0:T(8,128)(2,1)S(1)}, u32[]{:S(2)}, u32[]{:S(2)}) collective-permute-start(bf16[8,96,256]{2,1,0:T(8,128)(2,1)S(1)} %collective-permute-done.refs_1_), channel_id=1, source_target_pairs={{0,1},{1,0},{2,3},{3,2},{4,5},{5,4},{6,7},{7,6},{8,9},{9,8},{10,11... | collective-permute-start | bytes 1179656 | tf_op jit(solution)/shard_map/ppermute | solution.py:318
  65.8 0.0 collective-permute-done.10.refs_3_
  65.8 0.1 collective-permute-start.7
  65.9 0.0 collective-permute-done.3.refs_3_
  65.9 0.4 collective-permute-start.8
  66.4 0.0 collective-permute-done.5.refs_4_
  66.4 0.1 collective-permute-start.9
  66.5 0.0 collective-permute-done.11.refs_4_
  66.5 11.1 %shard_map.48 = (bf16[6,128,256]{2,1,0:T(8,128)(2,1)S(1)}, f32[6,128,256]{2,1,0:T(8,128)S(1)}, f32[6,8,256]{2,1,0:T(8,128)S(1)}, bf16[6,128,256]{2,1,0:T(8,128)(...) custom-call(s32[32]{0:T(128)S(1)} %copy-done, bf16[8,96,256]{2,1,0:T(8,128)(2,1)S(1)} %collective-permute-done.2.refs_1_, ...), custom_call_target="tpu_custom_call" | custom-call | flops 4800000000 | bytes 4000000 | tf_op jit(solution)/shard_map/pallas_call | solution.py:228
  77.6 5.8 %shard_map.50 = (bf16[6,128,256]{2,1,0:T(8,128)(2,1)S(1)}, f32[6,128,256]{2,1,0:T(8,128)S(1)}, f32[6,8,256]{2,1,0:T(8,128)S(1)}) custom-call(s32[32]{0:T(128)S(1)} %copy-done, bf16[8,96,256]{2,1,0:T(8,128)(2,1)S(1)} %collective-permute-done.refs_1_, bf16[8,96,256]{2,1,0:T(8,128)(2,1)S(1)} %collective-permute-done.1.refs_2_, ...), custom_call_target="tpu_custom_call" | custom-call | flops 2400000000 | bytes 4000000 | tf_op jit(solution)/shard_map/pallas_call | solution.py:228
  83.4 0.0 collective-permute-done.6.refs_5_.refs_1_
  83.4 0.0 collective-permute-done.7.refs_6_.refs_2_
  83.4 0.0 collective-permute-done.8.refs_7_.refs_3_
  83.4 0.0 collective-permute-done.9.refs_8_.refs_4_
  83.4 7.2 %shard_map.51 = (bf16[768,128]{1,0:T(8,128)(2,1)S(1)}, bf16[768,128]{1,0:T(8,128)(2,1)S(1)}) custom-call(s32[32]{0:T(128)S(1)} %copy-done, bf16[8,96,256]{2,1,0:T(8,128)(2,1)S(1)} %collective-permute-done.6.refs_5_.refs_1_, bf16[8,96,256]{2,1,0:T(8,128)(2,1)S(1)} %collective-permute-done.7.refs_6_.refs_2_, ...), custom_call_target="tpu_custom_call" | custom-call | flops 2400000000 | bytes 4000000 | tf_op jit(solution)/shard_map/pallas_call | solution.py:228
  90.6 1.6 %collective-permute-start.16 = (bf16[768,128]{1,0:T(8,128)(2,1)S(1)}, bf16[768,128]{1,0:T(8,128)(2,1)S(1)}, u32[]{:S(2)}, u32[]{:S(2)}) collective-permute-start(bf16[768,128]{1,0:T(8,128)(2,1)S(1)} %get-tuple-element.43), channel_id=1, source_target_pairs={{0,8},{8,0},{1,9},{9,1},{2,10},{10,2},{3,11},{11,3},{4,12},{12,4},... | collective-permute-start | bytes 589832 | tf_op jit(solution)/shard_map/ppermute | solution.py:318
  92.2 2.1 %collective-permute-start.17 = (bf16[768,128]{1,0:T(8,128)(2,1)S(1)}, bf16[768,128]{1,0:T(8,128)(2,1)S(1)}, u32[]{:S(2)}, u32[]{:S(2)}) collective-permute-start(bf16[768,128]{1,0:T(8,128)(2,1)S(1)} %get-tuple-element.44), channel_id=1, source_target_pairs={{0,9},{1,8},{8,1},{9,0},{2,11},{3,10},{10,3},{11,2},{4,13},{5,12},... | collective-permute-start | bytes 589832 | tf_op jit(solution)/shard_map/ppermute | solution.py:318
  94.3 12.7 %shard_map.49 = (bf16[768,128]{1,0:T(8,128)(2,1)S(1)}, bf16[768,128]{1,0:T(8,128)(2,1)S(1)}) custom-call(s32[32]{0:T(128)S(1)} %copy-done, bf16[8,96,256]{2,1,0:T(8,128)(2,1)S(1)} %collective-permute-done.refs_1_, bf16[8,96,256]{2,1,0:T(8,128)(2,1)S(1)} %collective-permute-done.1.refs_2_, bf16[8,96,256]{2,1,0:T(8,128)(2,1)S(1)} %collective-permute-done.3.refs_3_, ...), custom_call_target="tpu_custom_call" | custom-call | flops 4800000000 | bytes 4000000 | tf_op jit(solution)/shard_map/pallas_call | solution.py:228
  107.0 0.1 collective-permute-start.15
  107.1 0.0 collective-permute-done.16.z_same
  107.1 0.0 collective-permute-done.17.z_cross
  107.1 1.4 %collective-permute-done.15.swapped = bf16[768,128]{1,0:T(8,128)(2,1)S(1)} collective-permute-done((bf16[768,128]{1,0:T(8,128)(2,1)S(1)}, bf16[768,128]{1,0:T(8,128)(2,1)S(1)}, u32[]{:S(2)}, u32[]{:S(2)}) %collective-permute-start.15) | collective-permute-done | bytes 196640 | tf_op jit(solution)/shard_map/ppermute | solution.py:318
  108.5 1.1 shard_map.52
Async XLA Ops:
  32.3 21.3 %copy-start = (s32[32]{0:T(128)S(1)}, s32[32]{0:T(128)}, u32[]{:S(2)}) copy-start(s32[32]{0:T(128)} %refs_0_.9) | copy-start | bytes 388
  32.5 4.3 %collective-permute-start.12 = (bf16[8,96,256]{2,1,0:T(8,128)(2,1)S(1)}, bf16[8,96,256]{2,1,0:T(8,128)(2,1)S(1)}, u32[]{:S(2)}, u32[]{:S(2)}) collective-permute-start(bf16[8,96,256]{2,1,0:T(8,128)(2,1)S(1)} %get-tuple-element.26.refs_1_), channel_id=1, source_target_pairs={{0,1},{1,0},{2,3},{3,2},{4,5},{5,4},{6,7},{7,6},{8,9},{9,8},{10,11... | collective-permute-start | bytes 1179656 | tf_op jit(solution)/shard_map/ppermute | solution.py:318
  34.6 3.2 %collective-permute-start.13 = (bf16[8,96,256]{2,1,0:T(8,128)(2,1)S(1)}, bf16[8,96,256]{2,1,0:T(8,128)(2,1)S(1)}, u32[]{:S(2)}, u32[]{:S(2)}) collective-permute-start(bf16[8,96,256]{2,1,0:T(8,128)(2,1)S(1)} %get-tuple-element.25.refs_2_), channel_id=1, source_target_pairs={{0,1},{1,0},{2,3},{3,2},{4,5},{5,4},{6,7},{7,6},{8,9},{9,8},{10,11... | collective-permute-start | bytes 1179656 | tf_op jit(solution)/shard_map/ppermute | solution.py:318
  34.7 10.3 %collective-permute-start.2 = (bf16[8,96,256]{2,1,0:T(8,128)(2,1)S(1)}, bf16[8,96,256]{2,1,0:T(8,128)(2,1)S(1)}, u32[]{:S(2)}, u32[]{:S(2)}) collective-permute-start(bf16[8,96,256]{2,1,0:T(8,128)(2,1)S(1)} %get-tuple-element.26.refs_1_), channel_id=1, source_target_pairs={{0,2},{2,4},{4,6},{6,0},{1,3},{3,5},{5,7},{7,1},{8,10},{10,12},{12... | collective-permute-start | bytes 1179656 | tf_op jit(solution)/shard_map/ppermute | solution.py:313
  35.6 11.5 %collective-permute-start.14 = (bf16[16,96,128]{2,1,0:T(8,128)(2,1)S(1)}, bf16[16,96,128]{2,1,0:T(8,128)(2,1)S(1)}, u32[]{:S(2)}, u32[]{:S(2)}) collective-permute-start(bf16[16,96,128]{2,1,0:T(8,128)(2,1)S(1)} %get-tuple-element.28), channel_id=1, source_target_pairs={{0,1},{1,0},{2,3},{3,2},{4,5},{5,4},{6,7},{7,6},{8,9},{9,8},{10,11... | collective-permute-start | bytes 1179656 | tf_op jit(solution)/shard_map/ppermute | solution.py:318
  36.3 11.7 %collective-permute-start.4 = (bf16[8,96,256]{2,1,0:T(8,128)(2,1)S(1)}, bf16[8,96,256]{2,1,0:T(8,128)(2,1)S(1)}, u32[]{:S(2)}, u32[]{:S(2)}) collective-permute-start(bf16[8,96,256]{2,1,0:T(8,128)(2,1)S(1)} %get-tuple-element.25.refs_2_), channel_id=1, source_target_pairs={{0,6},{2,0},{4,2},{6,4},{1,7},{3,1},{5,3},{7,5},{8,14},{10,8},{12,... | collective-permute-start | bytes 1179656 | tf_op jit(solution)/shard_map/ppermute | solution.py:313
  36.9 16.5 %collective-permute-start = (bf16[8,96,256]{2,1,0:T(8,128)(2,1)S(1)}, bf16[8,96,256]{2,1,0:T(8,128)(2,1)S(1)}, u32[]{:S(2)}, u32[]{:S(2)}) collective-permute-start(bf16[8,96,256]{2,1,0:T(8,128)(2,1)S(1)} %get-tuple-element.25.refs_2_), channel_id=1, source_target_pairs={{0,2},{2,4},{4,6},{6,0},{1,3},{3,5},{5,7},{7,1},{8,10},{10,12},{12... | collective-permute-start | bytes 1179656 | tf_op jit(solution)/shard_map/ppermute | solution.py:313
  37.8 25.5 %collective-permute-start.1 = (bf16[8,96,256]{2,1,0:T(8,128)(2,1)S(1)}, bf16[8,96,256]{2,1,0:T(8,128)(2,1)S(1)}, u32[]{:S(2)}, u32[]{:S(2)}) collective-permute-start(bf16[8,96,256]{2,1,0:T(8,128)(2,1)S(1)} %get-tuple-element.26.refs_1_), channel_id=1, source_target_pairs={{0,6},{2,0},{4,2},{6,4},{1,7},{3,1},{5,3},{7,5},{8,14},{10,8},{12,... | collective-permute-start | bytes 1179656 | tf_op jit(solution)/shard_map/ppermute | solution.py:313
  45.0 20.9 %collective-permute-start.10 = (bf16[8,96,256]{2,1,0:T(8,128)(2,1)S(1)}, bf16[8,96,256]{2,1,0:T(8,128)(2,1)S(1)}, u32[]{:S(2)}, u32[]{:S(2)}) collective-permute-start(bf16[8,96,256]{2,1,0:T(8,128)(2,1)S(1)} %collective-permute-done.2.refs_1_), channel_id=1, source_target_pairs={{0,1},{1,0},{2,3},{3,2},{4,5},{5,4},{6,7},{7,6},{8,9},{9,8},{10,11... | collective-permute-start | bytes 1179656 | tf_op jit(solution)/shard_map/ppermute | solution.py:318
  47.1 18.8 %collective-permute-start.3 = (bf16[8,96,256]{2,1,0:T(8,128)(2,1)S(1)}, bf16[8,96,256]{2,1,0:T(8,128)(2,1)S(1)}, u32[]{:S(2)}, u32[]{:S(2)}) collective-permute-start(bf16[8,96,256]{2,1,0:T(8,128)(2,1)S(1)} %collective-permute-done.2.refs_1_), channel_id=1, source_target_pairs={{0,2},{2,4},{4,6},{6,0},{1,3},{3,5},{5,7},{7,1},{8,10},{10,12},{12... | collective-permute-start | bytes 1179656 | tf_op jit(solution)/shard_map/ppermute | solution.py:313
  48.0 18.4 %collective-permute-start.11 = (bf16[8,96,256]{2,1,0:T(8,128)(2,1)S(1)}, bf16[8,96,256]{2,1,0:T(8,128)(2,1)S(1)}, u32[]{:S(2)}, u32[]{:S(2)}) collective-permute-start(bf16[8,96,256]{2,1,0:T(8,128)(2,1)S(1)} %collective-permute-done.4.refs_2_), channel_id=1, source_target_pairs={{0,1},{1,0},{2,3},{3,2},{4,5},{5,4},{6,7},{7,6},{8,9},{9,8},{10,11... | collective-permute-start | bytes 1179656 | tf_op jit(solution)/shard_map/ppermute | solution.py:318
  53.4 13.0 %collective-permute-start.5 = (bf16[8,96,256]{2,1,0:T(8,128)(2,1)S(1)}, bf16[8,96,256]{2,1,0:T(8,128)(2,1)S(1)}, u32[]{:S(2)}, u32[]{:S(2)}) collective-permute-start(bf16[8,96,256]{2,1,0:T(8,128)(2,1)S(1)} %collective-permute-done.4.refs_2_), channel_id=1, source_target_pairs={{0,6},{2,0},{4,2},{6,4},{1,7},{3,1},{5,3},{7,5},{8,14},{10,8},{12,... | collective-permute-start | bytes 1179656 | tf_op jit(solution)/shard_map/ppermute | solution.py:313
  63.3 20.1 %collective-permute-start.6 = (bf16[8,96,256]{2,1,0:T(8,128)(2,1)S(1)}, bf16[8,96,256]{2,1,0:T(8,128)(2,1)S(1)}, u32[]{:S(2)}, u32[]{:S(2)}) collective-permute-start(bf16[8,96,256]{2,1,0:T(8,128)(2,1)S(1)} %collective-permute-done.refs_1_), channel_id=1, source_target_pairs={{0,1},{1,0},{2,3},{3,2},{4,5},{5,4},{6,7},{7,6},{8,9},{9,8},{10,11... | collective-permute-start | bytes 1179656 | tf_op jit(solution)/shard_map/ppermute | solution.py:318
  65.8 17.6 %collective-permute-start.7 = (bf16[8,96,256]{2,1,0:T(8,128)(2,1)S(1)}, bf16[8,96,256]{2,1,0:T(8,128)(2,1)S(1)}, u32[]{:S(2)}, u32[]{:S(2)}) collective-permute-start(bf16[8,96,256]{2,1,0:T(8,128)(2,1)S(1)} %collective-permute-done.1.refs_2_), channel_id=1, source_target_pairs={{0,1},{1,0},{2,3},{3,2},{4,5},{5,4},{6,7},{7,6},{8,9},{9,8},{10,11... | collective-permute-start | bytes 1179656 | tf_op jit(solution)/shard_map/ppermute | solution.py:318
  65.9 17.5 %collective-permute-start.8 = (bf16[8,96,256]{2,1,0:T(8,128)(2,1)S(1)}, bf16[8,96,256]{2,1,0:T(8,128)(2,1)S(1)}, u32[]{:S(2)}, u32[]{:S(2)}) collective-permute-start(bf16[8,96,256]{2,1,0:T(8,128)(2,1)S(1)} %collective-permute-done.3.refs_3_), channel_id=1, source_target_pairs={{0,1},{1,0},{2,3},{3,2},{4,5},{5,4},{6,7},{7,6},{8,9},{9,8},{10,11... | collective-permute-start | bytes 1179656 | tf_op jit(solution)/shard_map/ppermute | solution.py:318
  66.4 17.1 %collective-permute-start.9 = (bf16[8,96,256]{2,1,0:T(8,128)(2,1)S(1)}, bf16[8,96,256]{2,1,0:T(8,128)(2,1)S(1)}, u32[]{:S(2)}, u32[]{:S(2)}) collective-permute-start(bf16[8,96,256]{2,1,0:T(8,128)(2,1)S(1)} %collective-permute-done.5.refs_4_), channel_id=1, source_target_pairs={{0,1},{1,0},{2,3},{3,2},{4,5},{5,4},{6,7},{7,6},{8,9},{9,8},{10,11... | collective-permute-start | bytes 1179656 | tf_op jit(solution)/shard_map/ppermute | solution.py:318
  90.6 16.5 %collective-permute-start.16 = (bf16[768,128]{1,0:T(8,128)(2,1)S(1)}, bf16[768,128]{1,0:T(8,128)(2,1)S(1)}, u32[]{:S(2)}, u32[]{:S(2)}) collective-permute-start(bf16[768,128]{1,0:T(8,128)(2,1)S(1)} %get-tuple-element.43), channel_id=1, source_target_pairs={{0,8},{8,0},{1,9},{9,1},{2,10},{10,2},{3,11},{11,3},{4,12},{12,4},... | collective-permute-start | bytes 589832 | tf_op jit(solution)/shard_map/ppermute | solution.py:318
  92.2 14.9 %collective-permute-start.17 = (bf16[768,128]{1,0:T(8,128)(2,1)S(1)}, bf16[768,128]{1,0:T(8,128)(2,1)S(1)}, u32[]{:S(2)}, u32[]{:S(2)}) collective-permute-start(bf16[768,128]{1,0:T(8,128)(2,1)S(1)} %get-tuple-element.44), channel_id=1, source_target_pairs={{0,9},{1,8},{8,1},{9,0},{2,11},{3,10},{10,3},{11,2},{4,13},{5,12},... | collective-permute-start | bytes 589832 | tf_op jit(solution)/shard_map/ppermute | solution.py:318
  107.0 1.5 %collective-permute-start.15 = (bf16[768,128]{1,0:T(8,128)(2,1)S(1)}, bf16[768,128]{1,0:T(8,128)(2,1)S(1)}, u32[]{:S(2)}, u32[]{:S(2)}) collective-permute-start(bf16[768,128]{1,0:T(8,128)(2,1)S(1)} %get-tuple-element.36), channel_id=1, source_target_pairs={{0,1},{1,0},{2,3},{3,2},{4,5},{5,4},{6,7},{7,6},{8,9},{9,8},{10,11... | collective-permute-start | bytes 589832 | tf_op jit(solution)/shard_map/ppermute | solution.py:318
